TPU v7x, 512 devices: a whole 4x8x8 slice. The times are simulated.
512 devices in a mesh: gx: 64 (over x, y, core), ta: 8 (over z).
Axes of the slice: x: 4, y: 8, z: 8, core: 2. Of those that a mesh axis runs over, the one named last changes fastest.
Arguments:
- master_flat: float32 [8388608], P(('gx', 'ta')), may hold values from -6 to 6
Outputs:
- serving_weight: bfloat16 [1, 8192, 1024], P(None, None, 'ta')
- channel_scale: float32 [1, 1024], P(None, 'ta')
All inputs are finite; a program needn't handle non-finite values.
Results may differ from a plain program's by a relative error of at most 0.015.
Values may be sent and summed in bfloat16 or wider, within the bound.
No kernel may reach another device: no remote copies, remote signals or barrier semaphores. Data moves between devices by JAX's collectives and lax.ppermute only.
A program may use at most 64 MiB of HBM per device.

v0:
```python
import jax
import jax.numpy as jnp
from jax import lax
from jax.sharding import PartitionSpec as P

D = 8192
KVH = 8
HEAD = 128
LAYERS = 1


def relayout(shard):
    regrouped = lax.all_to_all(shard, "ta", split_axis=1, concat_axis=0, tiled=True)
    complete = lax.all_gather(regrouped, "gx", axis=0, tiled=True)
    return complete.reshape(LAYERS, D, -1)


def shards(master_flat):
    kv_width = KVH * HEAD
    row_count = master_flat.shape[0] // kv_width
    rounded = master_flat.reshape(row_count, kv_width).astype(jnp.bfloat16)
    complete = relayout(rounded)
    widened = complete.astype(jnp.float32)
    channel_scale = jnp.max(jnp.abs(widened), axis=1)
    serving_weight = (widened / channel_scale[:, None, :]).astype(jnp.bfloat16)
    return (serving_weight, channel_scale)


def solution(mesh):
    in_specs = (P(("gx", "ta")),)
    out_specs = (P(None, None, "ta"), P(None, "ta"))
    return jax.shard_map(shards, mesh=mesh, in_specs=in_specs, out_specs=out_specs, check_vma=False)
```

profile of v0, /device:TPU:1, one launch (start us, length us, event | category | flops | bytes accessed | tf_op | source)
XLA Modules:
  0.0 117.4 jit_solution(15112434270394180846)
XLA Ops:
  7.2 0.0 all-gather.2.cloned.1.call-start
  7.2 0.8 convert_bitcast_fusion
  8.1 17.6 %all_to_all.16 = bf16[16,8,128]{2,0,1:T(8,128)(2,1)} all-to-all(bf16[16,8,128]{2,0,1:T(8,128)(2,1)S(1)} %copy.4), channel_id=1, replica_groups=mesh['gx'=64,'ta'=8] {'ta'}, dimensions={1} | all-to-all | bytes 65536 | tf_op jit(solution)/shard_map/all_to_all | solution.py:13
  25.7 0.0 all-gather.2.cloned.1.call-update
  25.7 80.8 %all-gather.2.cloned.1.call-done = bf16[8192,128]{1,0:T(8,128)(2,1)} async-done(((bf16[128,128]{1,0:T(8,128)(2,1)}), bf16[8192,128]{1,0:T(8,128)(2,1)}) %all-gather.2.cloned.1.call-update) | async-done | bytes 2097168 | tf_op jit(solution)/shard_map/all_gather | solution.py:14
  106.6 0.0 copy-start
  106.6 2.0 %fusion = f32[128]{0:T(128)S(1)} fusion(bf16[8192,128]{1,0:T(8,128)(2,1)} %all-gather.2.cloned.1.call-done), kind=kLoop, calls=%fused_computation.2 | loop fusion | flops 3145600 | bytes 2097664 | tf_op jit(solution)/shard_map/reduce_max | solution.py:24
  108.6 0.2 copy-done
  108.8 0.0 copy-start.1
  108.8 1.7 %fusion.2 = bf16[1,8192,128]{2,1,0:T(8,128)(2,1)} fusion(bf16[8192,128]{1,0:T(8,128)(2,1)S(1)} %copy-done, f32[128]{0:T(128)S(1)} %fusion), kind=kLoop, calls=%fused_computation.4 | loop fusion | flops 3145728 | bytes 4194816 | tf_op jit(solution)/shard_map/convert_element_type | solution.py:25
  110.5 0.0 copy-done.1
  (1 shorter events, 0.0 us)
Async XLA Ops:
  7.2 99.4 %all-gather.2.cloned.1.call-start = ((), (), s32[]{:S(2)}) async-start(), calls=%async_computation.1 | async-start | bytes 2129920 | tf_op jit(solution)/shard_map/all_gather | solution.py:14
  106.6 2.2 %copy-start = (bf16[8192,128]{1,0:T(8,128)(2,1)S(1)}, bf16[8192,128]{1,0:T(8,128)(2,1)}, u32[]{:S(2)}) copy-start(bf16[8192,128]{1,0:T(8,128)(2,1)} %all-gather.2.cloned.1.call-done) | copy-start | bytes 6291460
  108.8 1.7 %copy-start.1 = (f32[128]{0:T(128)}, f32[128]{0:T(128)S(1)}, u32[]{:S(2)}) copy-start(f32[128]{0:T(128)S(1)} %fusion) | copy-start | bytes 1540
Sparse Core Ops, SparseCore 0:
  25.8 80.6 all-gather.1
where the time goes:
time: 118 us; the launch traced here: 117 us
  waiting for transfers between devices  80.9 us (69%)
  blocking collectives  17.6 us (15%)
  between operations  14 us (12%)
  other arithmetic  4.6 us (4%)
    all_gather x1, waiting for transfers between devices, relayout(): complete = lax.all_gather(regrouped, 'gx', axis=0, tiled=True)  80.8 us
    all_to_all x1, blocking collectives, relayout(): lax.all_to_all(shard, 'ta', split_axis=1, concat_axis=0, tiled=True)  17.6 us
  transfers between devices with their start and end apart: 1, of which 1 were waited for; matrix products, arithmetic and copies ran while one was open for 0% of the time, Pallas kernels for 0%

commit v1 on v0

--- a/solution.py
+++ b/solution.py
@@ -9,9 +9,14 @@
 LAYERS = 1
 
 
+def tiled_gather(shard, axis, dim):
+    copies = jnp.concatenate([shard] * lax.axis_size(axis), axis=dim)
+    return lax.all_to_all(copies, axis, dim, dim, tiled=True)
+
+
 def relayout(shard):
     regrouped = lax.all_to_all(shard, "ta", split_axis=1, concat_axis=0, tiled=True)
-    complete = lax.all_gather(regrouped, "gx", axis=0, tiled=True)
+    complete = tiled_gather(regrouped, "gx", 0)
     return complete.reshape(LAYERS, D, -1)
 
 

time: 118 us -> 85.9 us (0.73)
  waiting for transfers between devices: 80.9 us -> 0 us
  blocking collectives: 17.6 us -> 80.8 us
  between operations: 14 us -> 0.95 us
  other arithmetic: 4.6 us -> 3.34 us
    all_gather x1 -> x0, waiting for transfers between devices: 80.8 us -> none  [relayout(): complete = lax.all_gather(regrouped, 'gx', axis=0, tiled=True)]
    all_to_all x0 -> x1, blocking collectives: none -> 63.2 us  [tiled_gather(): return lax.all_to_all(copies, axis, dim, dim, tiled=True)]
    reduce_max x1, other arithmetic: 2.03 us -> 0.32 us  [shards(): channel_scale = jnp.max(jnp.abs(widened), axis=1)]
  transfers between devices with their start and end apart: 1 -> 0, of which waited for: 1 -> 0; matrix products, arithmetic and copies ran while one was open for 0% -> 0% of each run, Pallas kernels for 0% -> 0%
where the time goes in v1:
time: 85.9 us; the launch traced here: 85.7 us
  blocking collectives  80.8 us (94%)
  other arithmetic  3.34 us (4%)
  between operations  0.95 us (1%)
    all_to_all x1, blocking collectives, tiled_gather(): return lax.all_to_all(copies, axis, dim, dim, tiled=True)  63.2 us
    all_to_all x1, blocking collectives, relayout(): lax.all_to_all(shard, 'ta', split_axis=1, concat_axis=0, tiled=True)  17.5 us

profile of v1, /device:TPU:1, one launch (start us, length us, event | category | flops | bytes accessed | tf_op | source)
XLA Modules:
  0.0 85.7 jit_solution(17836894372241991580)
XLA Ops:
  0.6 0.8 convert_bitcast_fusion
  1.5 17.5 %all_to_all.25 = bf16[16,8,128]{2,0,1:T(8,128)(2,1)S(1)} all-to-all(bf16[16,8,128]{2,0,1:T(8,128)(2,1)S(1)} %copy.4), channel_id=1, replica_groups=mesh['gx'=64,'ta'=8] {'ta'}, dimensions={1} | all-to-all | bytes 65536 | tf_op jit(solution)/shard_map/all_to_all | solution.py:18
  20.0 63.2 %all_to_all.26 = bf16[64,128,128]{2,1,0:T(8,128)(2,1)S(1)} all-to-all(bf16[64,128,128]{2,1,0:T(8,128)(2,1)S(1)} %bitcast.77), channel_id=1, replica_groups=mesh['gx'=64,'ta'=8] {'gx'}, dimensions={0} | all-to-all | bytes 4194304 | tf_op jit(solution)/shard_map/all_to_all | solution.py:14
  83.2 0.3 abs_reduce_fusion
  83.5 0.0 copy-start
  83.5 0.5 convert_element_type.42
  84.0 0.0 copy-done
  84.1 1.7 %fusion = bf16[1,8192,128]{2,1,0:T(8,128)(2,1)} fusion(f32[128]{0:T(128)S(1)} %abs_reduce_fusion, f32[1,8192,128]{2,1,0:T(8,128)S(1)} %bitcast.76), kind=kLoop, calls=%fused_computation.1 | loop fusion | flops 2097152 | bytes 6291968 | tf_op jit(solution)/shard_map/convert_element_type | solution.py:30
  (65 shorter events, 0.7 us)
Async XLA Ops:
  83.5 0.5 copy-start
